TPU v7x, 32 devices: a 4x4x1 block of a 4x4x8 slice. The times are simulated.
32 devices in a mesh: dp: 1 (over z), tp: 32 (over y, x, core).
Axes of the slice: x: 4, y: 4, z: 1, core: 2. Of those that a mesh axis runs over, the one named last changes fastest.
The devices are a block of a 4x4x8 slice.
Arguments:
- x_in: bfloat16 [512, 4096], P('dp')
- lengths: int32 [512], P('dp')
- norm_gain: bfloat16 [2, 4096], replicated
- w_q: bfloat16 [2, 4096, 4096], P(None, None, 'tp')
- w_k: bfloat16 [2, 4096, 4096], P(None, None, 'tp')
- w_v: bfloat16 [2, 4096, 4096], P(None, None, 'tp')
- w_o: bfloat16 [2, 4096, 4096], P(None, 'tp')
- w_gate: bfloat16 [2, 4096, 11008], P(None, None, 'tp')
- w_up: bfloat16 [2, 4096, 11008], P(None, None, 'tp')
- w_down: bfloat16 [2, 11008, 4096], P(None, 'tp')
- k_cache: bfloat16 [2, 512, 32, 32, 128], P(None, 'dp', None, 'tp')
- v_cache: bfloat16 [2, 512, 32, 32, 128], P(None, 'dp', None, 'tp')
Outputs:
- output: bfloat16 [512, 4096], P('dp')
All inputs are finite; a program needn't handle non-finite values.
Results may differ from a plain program's by a relative error of at most 0.0175018.
Values are sent between devices in bfloat16 or wider.
A program may use at most 768 MiB of HBM per device.

v0:
```python
import functools
import math

import jax
import jax.numpy as jnp
from jax import lax
from jax.experimental import pallas as pl
from jax.experimental.pallas import tpu as pltpu
from jax.sharding import PartitionSpec as P

NORM_EPS = 1e-5
ROPE_BASE = 500000.0
F32 = jnp.float32
BF16 = jnp.bfloat16
NT = (((1,), (1,)), ((), ()))
BLOCKS = 2
TILE = 256


def wait_bytes(ref, sem):
    pltpu.make_async_copy(ref, ref, sem).wait()


def layers_kernel(side, x_hbm, len_ref, cos_ref, sin_ref, gain_ref, wq, wk, wv, wo, wg, wu, wd, kc, vc, out_ref,
                  a_buf, wqkv, wgu, wod, kbuf, vbuf, q_s, k_s, v_s, self_s, h_buf, send, recv, x_own, st_send, st_recv,
                  x_sem, w_sem, wo_sem, wp_ssem, wp_rsem, c_sem, own_sem, h_ssem, h_rsem, rs_ssem, rs_rsem, st_sem, ag_ssem, ag_rsem, d_ssem, d_rsem):
    layers, width = wq.shape[0], wq.shape[1]
    head = wq.shape[2]
    ff = wd.shape[1]
    half = width // 2
    quarter = width // 4
    toks = x_hbm.shape[3]
    chips = side * side
    rows = chips * toks
    seq = kc.shape[1] // (BLOCKS * rows)
    ff_tiles = wgu.shape[1] // TILE
    kdim = h_buf.shape[3]
    scale = head ** -0.5

    me = lax.axis_index('tp')
    core = lax.rem(me, 2)
    chip = lax.div(me, 2)
    px = lax.rem(chip, side)
    py = lax.div(chip, side)
    other = 1 - core

    def dev(y, x, c):
        return {'tp': (y * side + x) * 2 + c}

    def shift(p, d):
        return lax.rem(p + d + side, side)

    partner = dev(py, px, other)
    my_cols = pl.ds(pl.multiple_of(core * half, half), half)
    other_cols = pl.ds(pl.multiple_of(other * half, half), half)

    def part_cols(hf, c):
        return pl.ds(pl.multiple_of(c * half + hf * quarter, quarter), quarter)

    def k_rows(c, start, n):
        return pl.ds(pl.multiple_of(c * kdim + start, 8), n)

    def x_load(b):
        return pltpu.make_async_copy(x_hbm.at[b], out_ref.at[b], x_sem.at[b])

    def qkv_loads(l):
        return [pltpu.make_async_copy(w.at[l], wqkv.at[l, :, pl.ds(i * head, head)], w_sem.at[l, i]) for i, w in enumerate((wq, wk, wv))]

    def gu_loads(l):
        cps = []
        for j in range(ff_tiles):
            n = min(head, ff - j * head)
            for i, w in enumerate((wg, wu)):
                cps.append(pltpu.make_async_copy(w.at[l, pl.ds(j * head, n)], wgu.at[l, pl.ds(j * TILE + i * head, n)], w_sem.at[l, 3 + 2 * j + i]))
        return cps

    def od_own(l):
        return [
            pltpu.make_async_copy(wo.at[l, :, my_cols], wod.at[l, k_rows(core, 0, head)], wo_sem.at[l, 0]),
            pltpu.make_async_copy(wd.at[l, :, my_cols], wod.at[l, k_rows(core, head, ff)], wo_sem.at[l, 1]),
        ]

    def od_partner(l):
        return [
            pltpu.make_async_remote_copy(wo.at[l, :, other_cols], wod.at[l, k_rows(core, 0, head)], wp_ssem.at[l, 0], wp_rsem.at[l, 0], device_id=partner),
            pltpu.make_async_remote_copy(wd.at[l, :, other_cols], wod.at[l, k_rows(core, head, ff)], wp_ssem.at[l, 1], wp_rsem.at[l, 1], device_id=partner),
        ]

    def cache_loads(l, b):
        span = pl.ds(b * rows * seq, rows * seq)
        return [
            pltpu.make_async_copy(kc.at[l, span], kbuf.at[b], c_sem.at[b, 0]),
            pltpu.make_async_copy(vc.at[l, span], vbuf.at[b], c_sem.at[b, 1]),
        ]

    def start(cps):
        for cp in cps:
            cp.start()

    def wait(cps):
        for cp in cps:
            cp.wait()

    start([x_load(0)])
    tail = ff - (ff_tiles - 1) * head
    for l in range(layers):
        for i in range(2):
            lo = (ff_tiles - 1) * TILE + i * head + tail // 16 * 16
            hi = (ff_tiles - 1) * TILE + (i + 1) * head
            wgu[l, lo:hi, :] = jnp.zeros((hi - lo, width), BF16)
            lo = i * kdim + (head + ff) // 16 * 16
            wod[l, lo:(i + 1) * kdim, :] = jnp.zeros(((i + 1) * kdim - lo, half), BF16)
    start(qkv_loads(0) + cache_loads(0, 0) + [x_load(1)] + gu_loads(0))
    bar = pltpu.get_barrier_semaphore()
    pl.semaphore_signal(bar, inc=1, device_id=partner)
    for k in range(1, chips):
        pl.semaphore_signal(bar, inc=1, device_id=dev(shift(py, k // side), shift(px, k % side), core))

    def norm_rows(b):
        def body(i, carry):
            y, x = lax.div(i, side), lax.rem(i, side)
            xv = out_ref[b, y, x].astype(F32)
            inv = lax.rsqrt(jnp.mean(xv * xv, axis=-1, keepdims=True) + NORM_EPS)
            a_buf[b, y, x] = (xv * inv * gain_ref[0]).astype(BF16)
            return carry
        lax.fori_loop(0, chips, body, 0, unroll=2)

    wait([x_load(0)])
    start(od_own(0))
    norm_rows(0)
    pl.semaphore_wait(bar, chips)
    start(od_partner(0))
    start(cache_loads(0, 1))
    for b in range(BLOCKS):
        start([pltpu.make_async_copy(x_hbm.at[b, py, px, :, my_cols], x_own.at[b], own_sem.at[b])])

    def compute(l, b):
        if b == 0:
            wait(qkv_loads(l))
        if l == 0 and b == 1:
            wait([x_load(1)])
            norm_rows(1)
        r0 = b * rows
        a = a_buf[b].reshape(rows, width)
        qkv = jnp.dot(a, wqkv[l], preferred_element_type=F32).astype(BF16)
        cosv, sinv = cos_ref[r0:r0 + rows, :], sin_ref[r0:r0 + rows, :]

        def rope(v):
            v = v.astype(F32)
            return (v * cosv + pltpu.roll(v, head // 2, 1) * sinv).astype(BF16)

        qr, kr = rope(qkv[:, :head]), rope(qkv[:, head:2 * head])
        q_s[...] = qr
        v_s[...] = qkv[:, 2 * head:]
        self_s[...] = jnp.sum(qr.astype(F32) * kr.astype(F32), axis=-1, keepdims=True) * scale
        yield
        if b == 0:
            wait(gu_loads(l))
        if l + b > 0:
            wait_send_h(b, l)
        for j in range(ff_tiles):
            gu = lax.dot_general(a_buf[b].reshape(rows, width), wgu[l, j * TILE:(j + 1) * TILE, :], NT, preferred_element_type=F32)
            gate = gu[:, :head].astype(BF16).astype(F32)
            up = gu[:, head:].astype(BF16).astype(F32)
            h_buf[b, core, :, (j + 1) * head:(j + 2) * head] = (gate * jax.nn.sigmoid(gate) * up).astype(BF16)
            yield
        wait(cache_loads(l, b))
        grp = 16
        row_id = lax.broadcasted_iota(jnp.int32, (grp, grp * seq), 0)
        dist = lax.broadcasted_iota(jnp.int32, (grp, grp * seq), 1) - row_id * seq

        def attend(g):
            sl = pl.ds(pl.multiple_of(g * grp, grp), grp)
            ks = pl.ds(pl.multiple_of(g * grp * seq, grp * seq), grp * seq)
            lens = len_ref[pl.ds(pl.multiple_of(r0 + g * grp, grp), grp), :]
            logits = lax.dot_general(q_s[sl, :], kbuf[b, ks, :], NT, preferred_element_type=F32) * scale
            logits = jnp.where((dist >= 0) & (dist < lens), logits, -jnp.inf)
            own = self_s[sl, :]
            peak = jnp.maximum(jnp.max(logits, axis=-1, keepdims=True), own)
            w = jnp.exp(logits - peak)
            own_w = jnp.exp(own - peak)
            inv = 1.0 / (jnp.sum(w, axis=-1, keepdims=True) + own_w)
            p = (w * inv).astype(BF16)
            own_p = (own_w * inv).astype(BF16).astype(F32)
            o = jnp.dot(p, vbuf[b, ks, :], preferred_element_type=F32) + own_p * v_s[sl, :].astype(F32)
            h_buf[b, core, sl, 0:head] = o.astype(BF16)

        unroll = 4

        def attend_some(i, carry):
            for u in range(unroll):
                attend(i * unroll + u)
            return carry

        lax.fori_loop(0, rows // grp // unroll, attend_some, 0)
        h_send(b).start()
        if l + 1 < layers:
            start(cache_loads(l + 1, b))
        yield
        if b == 0:
            wait(od_own(l))
            for cp in od_partner(l):
                cp.wait_recv()
        if l > 0:
            wait_send_rs(b)
        h_recv_wait(b)
        for j in range(half // TILE):
            cols = slice(j * TILE, (j + 1) * TILE)
            y = jnp.dot(h_buf[b, 0], wod[l, 0:kdim, cols], preferred_element_type=F32) + jnp.dot(h_buf[b, 1], wod[l, kdim:2 * kdim, cols], preferred_element_type=F32)
            send[b, :, :, :, cols] = y.astype(BF16).reshape(side, side, toks, TILE)
        for k in far_first:
            rs_copy(b, k).start()
        yield

    def h_send(b):
        return pltpu.make_async_remote_copy(h_buf.at[b, core], h_buf.at[b, core], h_ssem.at[b], h_rsem.at[b], device_id=partner)

    def h_recv_wait(b):
        wait_bytes(h_buf.at[b, other], h_rsem.at[b])

    def wait_send_h(b, l):
        if l > 0:
            wait_bytes(h_buf.at[b, core], h_ssem.at[b])

    def ring_dist(d):
        return min(d, side - d)

    far_first = sorted(range(1, chips), key=lambda k: -(ring_dist(k // side) + ring_dist(k % side)))

    def rs_copy(b, k):
        ty, tx = shift(py, k // side), shift(px, k % side)
        return pltpu.make_async_remote_copy(send.at[b, ty, tx], recv.at[b, k - 1], rs_ssem.at[b], rs_rsem.at[b], device_id=dev(ty, tx, core))

    def wait_send_rs(b):
        wait_bytes(recv.at[b], rs_ssem.at[b])

    def st_copy(b):
        return pltpu.make_async_remote_copy(st_send.at[b], st_recv.at[b], st_sem.at[b, 0], st_sem.at[b, 1], device_id=partner)

    def finish(l, b):
        last = l + 1 == layers
        buf = out_ref if last else a_buf
        if l == 0:
            wait_bytes(x_own.at[b], own_sem.at[b])
        wait_bytes(recv.at[b], rs_rsem.at[b])
        sq = jnp.zeros((toks, 128), F32)
        chunk = 256
        for c0 in range(0, half, chunk):
            cols = slice(c0, c0 + chunk)
            acc = send[b, py, px, :, cols].astype(F32)
            for k in range(chips - 1):
                acc = acc + recv[b, k, :, cols].astype(F32)
            xn = (x_own[b, :, cols].astype(F32) + acc).astype(BF16)
            if last:
                buf[b, py, px, :, pl.ds(pl.multiple_of(core * half + c0, chunk), chunk)] = xn
            else:
                x_own[b, :, cols] = xn
                xf = xn.astype(F32)
                for i in range(chunk // 128):
                    v = xf[:, i * 128:(i + 1) * 128]
                    sq = sq + v * v
        if not last:
            if l > 0:
                st_copy(b).wait_send()
            st_send[b] = sq
            st_copy(b).start()
            yield
            st_copy(b).wait_recv()
            total = jnp.sum(st_send[b] + st_recv[b], axis=-1, keepdims=True)
            inv = lax.rsqrt(total / width + NORM_EPS)
            for c0 in range(0, half, chunk):
                cc = pl.ds(pl.multiple_of(core * half + c0, chunk), chunk)
                buf[b, py, px, :, cc] = (x_own[b, :, c0:c0 + chunk].astype(F32) * inv * gain_ref[l + 1, :, cc]).astype(BF16)
        sgn = 1 - 2 * core

        def place(hf, p1, p2=None):
            first = slice(None) if p1 is None else p1
            y, x = (p2, first) if hf == 0 else (first, p2)
            return buf.at[b, y, x, :, part_cols(hf, core)]

        def pos(hf):
            return (px, py) if hf == 0 else (py, px)

        def at(hf, p1, p2):
            return dev(p2, p1, core) if hf == 0 else dev(p1, p2, core)

        def copy(hf, ref, target, idx):
            return pltpu.make_async_remote_copy(ref, ref, ag_ssem.at[b, hf, idx], ag_rsem.at[b, hf, idx], device_id=target)

        def to_partner(hf, ref, idx):
            return pltpu.make_async_remote_copy(ref, ref, d_ssem.at[b, hf, idx], d_rsem.at[b, hf, idx], device_id=partner)

        for idx, d in ((2, 2), (0, 1), (1, -1)):
            for hf in range(2):
                p1, p2 = pos(hf)
                copy(hf, place(hf, p1, p2), at(hf, shift(p1, d), p2), idx).start()
        yield
        for hf in range(2):
            p1, p2 = pos(hf)
            for idx, d in ((0, -1), (1, 1), (2, 2)):
                wait_bytes(place(hf, shift(p1, d), p2), ag_rsem.at[b, hf, idx])
            for idx, d in ((3, 1), (4, -1)):
                copy(hf, place(hf, None, p2), at(hf, p1, shift(p2, d)), idx).start()
            to_partner(hf, place(hf, None, p2), 0).start()
        yield
        for hf in range(2):
            p1, p2 = pos(hf)
            for near in (0, 1):
                pass
            src = shift(p2, -sgn)
            line = place(hf, None, src)
            wait_bytes(line, ag_rsem.at[b, hf, 3 + core])
            copy(hf, line, at(hf, p1, shift(p2, sgn)), 5).start()
            to_partner(hf, line, 1).start()
        yield
        for hf in range(2):
            p1, p2 = pos(hf)
            line = place(hf, None, shift(p2, sgn))
            wait_bytes(line, ag_rsem.at[b, hf, 4 - core])
            to_partner(hf, line, 2).start()
        yield
        for hf in range(2):
            p1, p2 = pos(hf)
            line = place(hf, None, shift(p2, 2))
            wait_bytes(line, ag_rsem.at[b, hf, 5])
            to_partner(hf, line, 3).start()
        yield
        for hf in range(2):
            p1, p2 = pos(hf)
            for idx in range(4):
                wait_bytes(place(hf, None, p2), d_rsem.at[b, hf, idx])
            for idx in range(3):
                wait_bytes(place(hf, p1, p2), ag_ssem.at[b, hf, idx])
            for idx in range(3, 6):
                wait_bytes(place(hf, None, p2), ag_ssem.at[b, hf, idx])
            for idx in range(4):
                wait_bytes(place(hf, None, p2), d_ssem.at[b, hf, idx])

    def run(gen):
        for _ in gen:
            pass

    def beside(main, background):
        for _ in main:
            next(background, None)
        run(background)

    run(compute(0, 0))
    start([cp for l in range(1, layers) for cp in qkv_loads(l) + gu_loads(l) + od_own(l) + od_partner(l)])
    run(compute(0, 1))
    for l in range(1, layers):
        run(finish(l - 1, 0))
        tail_gen = finish(l - 1, 1)
        next(tail_gen)
        next(tail_gen)
        beside(compute(l, 0), tail_gen)
        run(compute(l, 1))
    run(finish(layers - 1, 0))
    run(finish(layers - 1, 1))
    for l in range(layers):
        for cp in od_partner(l):
            cp.wait_send()
    for b in range(BLOCKS):
        wait_bytes(h_buf.at[b, core], h_ssem.at[b])
        wait_send_rs(b)
        if layers > 1:
            st_copy(b).wait_send()


def solution(mesh):
    tp_size = mesh.shape['tp']
    side = math.isqrt(tp_size // 2)
    arg_specs = (P('dp', None), P('dp'), P(), P(None, None, 'tp'), P(None, None, 'tp'), P(None, None, 'tp'), P(None, 'tp', None), P(None, None, 'tp'), P(None, None, 'tp'), P(None, 'tp', None), P(None, 'dp', None, 'tp', None), P(None, 'dp', None, 'tp', None))

    def per_device(x_in, lengths, norm_gain, w_q, w_k, w_v, w_o, w_gate, w_up, w_down, k_cache, v_cache):
        tok_rows, width = x_in.shape
        layers, _, head = w_q.shape
        ff = w_gate.shape[2]
        seq = k_cache.shape[2]
        chips = side * side
        rows = tok_rows // BLOCKS
        toks = rows // chips
        half = width // 2
        ff_tiles = -(-ff // head)
        kdim = head * (1 + ff_tiles)

        inv_freq = 1.0 / (ROPE_BASE ** (jnp.arange(0, head, 2).astype(F32) / head))
        angles = lengths.astype(F32)[:, None] * inv_freq[None, :]
        cos_ang, sin_ang = jnp.cos(angles), jnp.sin(angles)
        cos_full = jnp.concatenate([cos_ang, cos_ang], axis=-1)
        sin_full = jnp.concatenate([-sin_ang, sin_ang], axis=-1)

        any_spec = pl.BlockSpec(memory_space=pl.ANY)
        vmem_spec = pl.BlockSpec(memory_space=pltpu.VMEM)
        dma = pltpu.SemaphoreType.DMA
        out = pl.pallas_call(
            functools.partial(layers_kernel, side),
            out_shape=jax.ShapeDtypeStruct((BLOCKS, side, side, toks, width), BF16),
            in_specs=[any_spec] + [vmem_spec] * 4 + [any_spec] * 9,
            out_specs=vmem_spec,
            scratch_shapes=[
                pltpu.VMEM((BLOCKS, side, side, toks, width), BF16),
                pltpu.VMEM((layers, width, 3 * head), BF16),
                pltpu.VMEM((layers, ff_tiles * TILE, width), BF16),
                pltpu.VMEM((layers, 2 * kdim, half), BF16),
                pltpu.VMEM((BLOCKS, rows * seq, head), BF16),
                pltpu.VMEM((BLOCKS, rows * seq, head), BF16),
                pltpu.VMEM((rows, head), BF16),
                pltpu.VMEM((rows, head), BF16),
                pltpu.VMEM((rows, head), BF16),
                pltpu.VMEM((rows, 1), F32),
                pltpu.VMEM((BLOCKS, 2, rows, kdim), BF16),
                pltpu.VMEM((BLOCKS, side, side, toks, half), BF16),
                pltpu.VMEM((BLOCKS, chips - 1, toks, half), BF16),
                pltpu.VMEM((BLOCKS, toks, half), BF16),
                pltpu.VMEM((BLOCKS, toks, 128), F32),
                pltpu.VMEM((BLOCKS, toks, 128), F32),
                dma((BLOCKS,)),
                dma((layers, 3 + 2 * ff_tiles)),
                dma((layers, 2)),
                dma((layers, 2)),
                dma((layers, 2)),
                dma((BLOCKS, 2)),
                dma((BLOCKS,)),
                dma((BLOCKS,)),
                dma((BLOCKS,)),
                dma((BLOCKS,)),
                dma((BLOCKS,)),
                dma((BLOCKS, 2)),
                dma((BLOCKS, 2, 6)),
                dma((BLOCKS, 2, 6)),
                dma((BLOCKS, 2, 4)),
                dma((BLOCKS, 2, 4)),
            ],
            compiler_params=pltpu.CompilerParams(collective_id=0, has_side_effects=True, vmem_limit_bytes=67043328),
            name='decoder_layers',
        )(
            x_in.reshape(BLOCKS, side, side, toks, width),
            lengths.reshape(tok_rows, 1),
            cos_full,
            sin_full,
            norm_gain.astype(F32).reshape(layers, 1, width),
            w_q, w_k, w_v, w_o,
            w_gate.swapaxes(1, 2),
            w_up.swapaxes(1, 2),
            w_down,
            k_cache.reshape(layers, tok_rows * seq, head),
            v_cache.reshape(layers, tok_rows * seq, head),
        )
        return out.reshape(tok_rows, width)

    return jax.shard_map(per_device, mesh=mesh, in_specs=arg_specs, out_specs=P('dp', None), check_vma=False)
```

profile of v0, /device:TPU:97, one launch (start us, length us, event | category | flops | bytes accessed | tf_op | source)
XLA Modules:
  0.0 164.0 jit_solution(5545076336574323557)
XLA Ops:
  0.0 0.7 convert_element_type.11
  0.7 1.3 reshape.37.gain_ref
  2.0 1.5 copy.13.len_ref
  3.6 1.0 fusion
  4.6 1.0 pad_maximum_fusion
  5.6 153.7 %decoder_layers.1 = bf16[2,4,4,16,4096]{4,3,2,1,0:T(8,128)(2,1)} custom-call(bf16[2,4,4,16,4096]{4,3,2,1,0:T(8,128)(2,1)} %bitcast.12, s32[512,1]{1,0:T(8,128)} %copy.13.len_ref, f32[512,128]{1,0:T(8,128)} %get-tuple-element.8.cos_ref, f32[512,128]{1,0:T(8,128)} %get-tuple-element.9.sin_ref, f32[2,1,4096]{2,1,0:T(1,128)} %reshape.37.gain_ref, ...), custom_call_target="tpu_custom_call" | custom-call | tf_op jit(solution)/shard_map/decoder_layers/pallas_call | solution.py:396
  159.3 4.7 %copy.15 = bf16[512,4096]{1,0:T(8,128)(2,1)} copy(bf16[512,4096]{1,0:T(8,128)(2,1)} %bitcast.7) | data formatting | bytes 8388608
  (1 shorter events, 0.0 us)
where the time goes:
time: 164 us
  Pallas kernels  154 us (94%)
  local copies, waits for them, and re-layouts  7.57 us (5%)
  other arithmetic  2.69 us (2%)
    pallas_call x1, Pallas kernels, per_device(): pl.pallas_call(functools.partial(layers_kernel, side), out_shape=jax.Shap...  154 us
    unnamed x1, local copies, waits for them, and re-layouts  4.7 us

commit v1 on v0

v1 whole, which is shorter than its diff:
```python
import functools
import math

import jax
import jax.numpy as jnp
import numpy as np
from jax import lax
from jax.experimental import pallas as pl
from jax.experimental.pallas import tpu as pltpu
from jax.sharding import PartitionSpec as P

NORM_EPS = 1e-5
ROPE_BASE = 500000.0
F32 = jnp.float32
BF16 = jnp.bfloat16
NT = (((1,), (1,)), ((), ()))
BLOCKS = 2
TILE = 256


def wait_bytes(ref, sem):
    pltpu.make_async_copy(ref, ref, sem).wait()


def layers_kernel(side, x_hbm, len_hbm, freq_hbm, gain_hbm, wq, wk, wv, wo, wg, wu, wd, kc, vc, out_hbm,
                  len_in, freq_ref, gain_ref, out_ref, len_ref, cos_ref, sin_ref, lg_s, pr_s, ow_s, a_buf, wqkv, wgu, wod, kbuf, vbuf, q_s, v_s, self_s, h_buf, send, r1, mid, r2, x_own, st_send, st_recv,
                  small_sem, x_sem, w_sem, wo_sem, wp_ssem, wp_rsem, c_sem, own_sem, h_ssem, h_rsem, p1_ssem, p1_rsem, p2_ssem, p2_rsem, st_sem, ag_ssem, ag_rsem, d_ssem, d_rsem, out_sem):
    layers, width = wq.shape[0], wq.shape[1]
    head = wq.shape[2]
    ff = wd.shape[1]
    half = width // 2
    quarter = width // 4
    toks = x_hbm.shape[3]
    chips = side * side
    rows = chips * toks
    seq = kc.shape[1] // (BLOCKS * rows)
    ff_tiles = wgu.shape[1] // TILE
    kdim = h_buf.shape[3]
    scale = head ** -0.5

    me = lax.axis_index('tp')
    core = lax.rem(me, 2)
    chip = lax.div(me, 2)
    px = lax.rem(chip, side)
    py = lax.div(chip, side)
    other = 1 - core

    def dev(y, x, c):
        return {'tp': (y * side + x) * 2 + c}

    def shift(p, d):
        return lax.rem(p + d + side, side)

    partner = dev(py, px, other)
    my_cols = pl.ds(pl.multiple_of(core * half, half), half)
    other_cols = pl.ds(pl.multiple_of(other * half, half), half)

    def part_cols(hf, c):
        return pl.ds(pl.multiple_of(c * half + hf * quarter, quarter), quarter)

    def k_rows(c, start, n):
        return pl.ds(pl.multiple_of(c * kdim + start, 8), n)

    def x_load(b):
        return pltpu.make_async_copy(x_hbm.at[b], out_ref.at[b], x_sem.at[b])

    def qkv_loads(l):
        return [pltpu.make_async_copy(w.at[l], wqkv.at[l, :, pl.ds(i * head, head)], w_sem.at[l, i]) for i, w in enumerate((wq, wk, wv))]

    def gu_loads(l):
        cps = []
        for j in range(ff_tiles):
            n = min(head, ff - j * head)
            for i, w in enumerate((wg, wu)):
                cps.append(pltpu.make_async_copy(w.at[l, pl.ds(j * head, n)], wgu.at[l, pl.ds(j * TILE + i * head, n)], w_sem.at[l, 3 + 2 * j + i]))
        return cps

    def od_own(l):
        return [
            pltpu.make_async_copy(wo.at[l, :, my_cols], wod.at[l, k_rows(core, 0, head)], wo_sem.at[l, 0]),
            pltpu.make_async_copy(wd.at[l, :, my_cols], wod.at[l, k_rows(core, head, ff)], wo_sem.at[l, 1]),
        ]

    def od_partner(l):
        return [
            pltpu.make_async_remote_copy(wo.at[l, :, other_cols], wod.at[l, k_rows(core, 0, head)], wp_ssem.at[l, 0], wp_rsem.at[l, 0], device_id=partner),
            pltpu.make_async_remote_copy(wd.at[l, :, other_cols], wod.at[l, k_rows(core, head, ff)], wp_ssem.at[l, 1], wp_rsem.at[l, 1], device_id=partner),
        ]

    def cache_loads(l, b):
        span = pl.ds(b * rows * seq, rows * seq)
        return [
            pltpu.make_async_copy(kc.at[l, span], kbuf.at[b], c_sem.at[b, 0]),
            pltpu.make_async_copy(vc.at[l, span], vbuf.at[b], c_sem.at[b, 1]),
        ]

    def start(cps):
        for cp in cps:
            cp.start()

    def wait(cps):
        for cp in cps:
            cp.wait()

    smalls = [pltpu.make_async_copy(src, dst, small_sem.at[i]) for i, (src, dst) in enumerate(((gain_hbm, gain_ref), (len_hbm, len_in), (freq_hbm, freq_ref)))]
    start(smalls + [x_load(0)] + qkv_loads(0))
    bar = pltpu.get_barrier_semaphore()

    def norm_rows(b):
        def body(i, carry):
            y, x = lax.div(i, side), lax.rem(i, side)
            xv = out_ref[b, y, x].astype(F32)
            inv = lax.rsqrt(jnp.mean(xv * xv, axis=-1, keepdims=True) + NORM_EPS)
            a_buf[b, y, x] = (xv * inv * gain_ref[0:1, :].astype(F32)).astype(BF16)
            return carry
        lax.fori_loop(0, chips, body, 0, unroll=2)

    tail = ff - (ff_tiles - 1) * head
    with jax.named_scope('zeros'):
        for l in range(layers):
            for i in range(2):
                lo = (ff_tiles - 1) * TILE + i * head + tail // 16 * 16
                hi = (ff_tiles - 1) * TILE + (i + 1) * head
                wgu[l, lo:hi, :] = jnp.zeros((hi - lo, width), BF16)
                lo = i * kdim + (head + ff) // 16 * 16
                wod[l, lo:(i + 1) * kdim, :] = jnp.zeros(((i + 1) * kdim - lo, half), BF16)
    pl.semaphore_signal(bar, inc=1, device_id=partner)
    for k in range(1, chips):
        pl.semaphore_signal(bar, inc=1, device_id=dev(shift(py, k // side), shift(px, k % side), core))
    with jax.named_scope('wait_x'):
        wait(smalls + [x_load(0)])
    start(gu_loads(0) + cache_loads(0, 0) + od_own(0))
    with jax.named_scope('norm_00'):
        norm_rows(0)
    with jax.named_scope('tables'):
        lane = lax.broadcasted_iota(jnp.int32, (128, head), 1)
        for i in range(len_in.shape[0]):
            pos_rows = jnp.broadcast_to(len_in[i:i + 1, :].astype(F32), (128, 128)).T
            len_ref[i * 128:(i + 1) * 128, :] = pos_rows[:, 0:1].astype(jnp.int32)
            angle = pos_rows[:, 0:head] * freq_ref[...]
            cos_ref[i * 128:(i + 1) * 128, :] = jnp.cos(angle)
            sin = jnp.sin(angle)
            sin_ref[i * 128:(i + 1) * 128, :] = jnp.where(lane < head // 2, -sin, sin)

    def enter():
        with jax.named_scope('barrier'):
            pl.semaphore_wait(bar, chips)
        start(od_partner(0))
        for l in range(1, layers):
            start(qkv_loads(l) + gu_loads(l) + od_own(l) + od_partner(l))

    for b in range(1, BLOCKS):
        start([x_load(b)] + cache_loads(0, b))
    for b in range(BLOCKS):
        start([pltpu.make_async_copy(x_hbm.at[b, py, px, :, my_cols], x_own.at[b], own_sem.at[b])])

    part = rows / 256

    def chain(b):
        for l in range(layers):
            yield from compute(l, b)
            yield from finish(l, b)

    def compute(l, b):
        if b == 0:
            with jax.named_scope(f'wait_qkv_{l}{b}'):
                wait(qkv_loads(l))
        if l == 0 and b > 0:
            with jax.named_scope(f'norm_{l}{b}'):
                wait([x_load(b)])
                norm_rows(b)
        r0 = b * rows
        with jax.named_scope(f'qkv_{l}{b}'):
            a = a_buf[b].reshape(rows, width)
            qkv = jnp.dot(a, wqkv[l], preferred_element_type=F32).astype(BF16)
            cosv, sinv = cos_ref[r0:r0 + rows, :], sin_ref[r0:r0 + rows, :]

            def rope(v):
                v = v.astype(F32)
                return (v * cosv + pltpu.roll(v, head // 2, 1) * sinv).astype(BF16)

            qr, kr = rope(qkv[:, :head]), rope(qkv[:, head:2 * head])
            q_s[b] = qr
            v_s[b] = qkv[:, 2 * head:]
            self_s[b] = jnp.sum(qr.astype(F32) * kr.astype(F32), axis=-1, keepdims=True) * scale
        yield 1.5 * part + (1.5 * part if l == 0 else 0), 0, 0, False
        if l == 0 and b == 0:
            enter()
        with jax.named_scope(f'wait_gu_{l}{b}'):
            if b == 0:
                wait(gu_loads(l))
        if l > 0:
            for i in range(2):
                h_send(b, i).wait_send()
        for j in range(ff_tiles):
            with jax.named_scope(f'gu_{l}{b}'):
                gu = lax.dot_general(a_buf[b].reshape(rows, width), wgu[l, j * TILE:(j + 1) * TILE, :], NT, preferred_element_type=F32)
                gate = gu[:, :head].astype(BF16).astype(F32)
                up = gu[:, head:].astype(BF16).astype(F32)
                h_buf[b, core, :, (j + 1) * head:(j + 2) * head] = (gate * jax.nn.sigmoid(gate) * up).astype(BF16)
            if j + 1 == ff_tiles:
                h_send(b, 1).start()
            yield 0.8 * part, 0, 0, False
        with jax.named_scope(f'wait_cache_{l}{b}'):
            wait(cache_loads(l, b))
        grp = 16
        unroll = 4
        span = 64

        def group(g):
            return pl.ds(pl.multiple_of(g * grp, grp), grp), pl.ds(pl.multiple_of(g * grp * seq, grp * seq), grp * seq)

        def score(i, carry):
            for u in range(unroll):
                sl, ks = group(i * unroll + u)
                lg_s[b, sl, :] = lax.dot_general(q_s[b, sl, :], kbuf[b, ks, :], NT, preferred_element_type=F32)
            return carry

        def soften(i, carry):
            sl = pl.ds(pl.multiple_of(i * span, span), span)
            lens = len_ref[pl.ds(pl.multiple_of(r0 + i * span, span), span), :]
            row_id = lax.rem(lax.broadcasted_iota(jnp.int32, (span, grp * seq), 0), grp)
            dist = lax.broadcasted_iota(jnp.int32, (span, grp * seq), 1) - row_id * seq
            logits = jnp.where((dist >= 0) & (dist < lens), lg_s[b, sl, :] * scale, -jnp.inf)
            own = self_s[b, sl, :]
            peak = jnp.maximum(jnp.max(logits, axis=-1, keepdims=True), own)
            w = jnp.exp(logits - peak)
            own_w = jnp.exp(own - peak)
            inv = 1.0 / (jnp.sum(w, axis=-1, keepdims=True) + own_w)
            pr_s[b, sl, :] = (w * inv).astype(BF16)
            ow_s[b, sl, :] = (own_w * inv).astype(BF16).astype(F32)
            return carry

        def mix(i, carry):
            for u in range(unroll):
                sl, ks = group(i * unroll + u)
                o = jnp.dot(pr_s[b, sl, :], vbuf[b, ks, :], preferred_element_type=F32) + ow_s[b, sl, :] * v_s[b, sl, :].astype(F32)
                h_buf[b, core, sl, 0:head] = o.astype(BF16)
            return carry

        with jax.named_scope(f'score_{l}{b}'):
            lax.fori_loop(0, rows // grp // unroll, score, 0)
        with jax.named_scope(f'soften_{l}{b}'):
            lax.fori_loop(0, rows // span, soften, 0)
        with jax.named_scope(f'mix_{l}{b}'):
            lax.fori_loop(0, rows // grp // unroll, mix, 0)
        h_send(b, 0).start()
        if l + 1 < layers:
            start(cache_loads(l + 1, b))
        yield 3.4 * part, 0, 1.5, False
        with jax.named_scope(f'wait_down_{l}{b}'):
            if b == 0:
                wait(od_own(l))
                for cp in od_partner(l):
                    cp.wait_recv()
            for i in range(2):
                h_send(b, i).wait_recv()
        for hf in range(2):
            with jax.named_scope(f'down_{l}{b}'):
                if l > 0:
                    for k in range(1, side):
                        p1_copy(b, hf, k).wait_send()
                for j in range(hf * quarter // TILE, (hf + 1) * quarter // TILE):
                    cols = slice(j * TILE, (j + 1) * TILE)
                    y = jnp.dot(h_buf[b, 0], wod[l, 0:kdim, cols], preferred_element_type=F32) + jnp.dot(h_buf[b, 1], wod[l, kdim:2 * kdim, cols], preferred_element_type=F32)
                    send[b, :, :, :, cols] = y.astype(BF16).reshape(side, side, toks, TILE)
                for k in far_first:
                    p1_copy(b, hf, k).start()
        yield 1.8 * part, 5.6 * part, 2.2, True

    def h_send(b, i):
        ref = h_buf.at[b, core, :, pl.ds(0, head)] if i == 0 else h_buf.at[b, core, :, pl.ds(head, kdim - head)]
        return pltpu.make_async_remote_copy(ref, ref, h_ssem.at[b, i], h_rsem.at[b, i], device_id=partner)

    far_first = sorted(range(1, side), key=lambda k: -min(k, side - k))

    def pos(hf):
        return (px, py) if hf == 0 else (py, px)

    def at(hf, p1, p2):
        return dev(p2, p1, core) if hf == 0 else dev(p1, p2, core)

    def line_of(ref, b, hf, p1, cols):
        return ref.at[b, :, p1, :, cols] if hf == 0 else ref.at[b, p1, :, :, cols]

    def hf_cols(hf):
        return pl.ds(hf * quarter, quarter)

    def p1_copy(b, hf, k):
        p1, p2 = pos(hf)
        to = shift(p1, k)
        return pltpu.make_async_remote_copy(line_of(send, b, hf, to, hf_cols(hf)), r1.at[b, hf, k - 1], p1_ssem.at[b, hf, k - 1], p1_rsem.at[b, hf, k - 1], device_id=at(hf, to, p2))

    def p2_copy(b, hf, k):
        p1, p2 = pos(hf)
        to = shift(p2, k)
        return pltpu.make_async_remote_copy(mid.at[b, hf, to], r2.at[b, hf, k - 1], p2_ssem.at[b, hf, k - 1], p2_rsem.at[b, hf, k - 1], device_id=at(hf, p1, to))

    def st_copy(b):
        return pltpu.make_async_remote_copy(st_send.at[b], st_recv.at[b], st_sem.at[b, 0], st_sem.at[b, 1], device_id=partner)

    def finish(l, b):
        last = l + 1 == layers
        buf = out_ref if last else a_buf
        if l == 0:
            wait_bytes(x_own.at[b], own_sem.at[b])
        chunk = 256
        for hf in range(2):
            p1, p2 = pos(hf)
            with jax.named_scope(f'wait_p1_{l}{b}'):
                for k in range(1, side):
                    p1_copy(b, hf, k).wait_recv()
                    if l > 0:
                        p2_copy(b, hf, k).wait_send()
            with jax.named_scope(f'mid_{l}{b}'):
                for q in range(side):
                    own = send[b, q, p1, :, hf * quarter:(hf + 1) * quarter] if hf == 0 else send[b, p1, q, :, hf * quarter:(hf + 1) * quarter]
                    acc = own.astype(F32)
                    for k in range(side - 1):
                        acc = acc + r1[b, hf, k, q].astype(F32)
                    mid[b, hf, q] = acc
                for k in far_first:
                    p2_copy(b, hf, k).start()
        yield 0.4 * part, 2.8 * part, 2.2, True
        sq = jnp.zeros((toks, 128), F32)
        for hf in range(2):
            p1, p2 = pos(hf)
            with jax.named_scope(f'wait_p2_{l}{b}'):
                for k in range(1, side):
                    p2_copy(b, hf, k).wait_recv()
            with jax.named_scope(f'reduce_{l}{b}'):
                for c0 in range(0, quarter, chunk):
                    cols = slice(c0, c0 + chunk)
                    xc = slice(hf * quarter + c0, hf * quarter + c0 + chunk)
                    acc = mid[b, hf, p2, :, cols]
                    for k in range(side - 1):
                        acc = acc + r2[b, hf, k, :, cols]
                    xn = (x_own[b, :, xc].astype(F32) + acc).astype(BF16)
                    if last:
                        buf[b, py, px, :, pl.ds(pl.multiple_of(core * half + hf * quarter + c0, chunk), chunk)] = xn
                    else:
                        x_own[b, :, xc] = xn
                        xf = xn.astype(F32)
                        for i in range(chunk // 128):
                            v = xf[:, i * 128:(i + 1) * 128]
                            sq = sq + v * v
        if not last:
            if l > 0:
                st_copy(b).wait_send()
            st_send[b] = sq
            st_copy(b).start()
            yield 0.2 * part, 0, 1.4, True
            with jax.named_scope(f'wait_st_{l}{b}'):
                st_copy(b).wait_recv()
            with jax.named_scope(f'scale_{l}{b}'):
                total = jnp.sum(st_send[b] + st_recv[b], axis=-1, keepdims=True)
                inv = lax.rsqrt(total / width + NORM_EPS)
                for c0 in range(0, half, chunk):
                    cc = pl.ds(pl.multiple_of(core * half + c0, chunk), chunk)
                    buf[b, py, px, :, cc] = (x_own[b, :, c0:c0 + chunk].astype(F32) * inv * gain_ref[l + 1:l + 2, cc].astype(F32)).astype(BF16)
        sgn = 1 - 2 * core

        def place(hf, p1, p2=None):
            first = slice(None) if p1 is None else p1
            y, x = (p2, first) if hf == 0 else (first, p2)
            return buf.at[b, y, x, :, part_cols(hf, core)]

        def copy(hf, ref, target, idx):
            return pltpu.make_async_remote_copy(ref, ref, ag_ssem.at[b, hf, idx], ag_rsem.at[b, hf, idx], device_id=target)

        def place_out(hf, c, p2, idx):
            y, x = (p2, slice(None)) if hf == 0 else (slice(None), p2)
            cols = part_cols(hf, c)
            return pltpu.make_async_copy(buf.at[b, y, x, :, cols], out_hbm.at[b, y, x, :, cols], out_sem.at[b, hf, idx])

        def to_partner(hf, ref, idx):
            return pltpu.make_async_remote_copy(ref, ref, d_ssem.at[b, hf, idx], d_rsem.at[b, hf, idx], device_id=partner)

        for idx, d in ((2, 2), (0, 1), (1, -1)):
            for hf in range(2):
                p1, p2 = pos(hf)
                copy(hf, place(hf, p1, p2), at(hf, shift(p1, d), p2), idx).start()
        yield 0.2, 1.4 * part, 2.6, True
        with jax.named_scope(f'gather1_{l}{b}'):
            for hf in range(2):
                p1, p2 = pos(hf)
                for idx, d in ((0, -1), (1, 1), (2, 2)):
                    wait_bytes(place(hf, shift(p1, d), p2), ag_rsem.at[b, hf, idx])
                for idx, d in ((3, 1), (4, -1)):
                    copy(hf, place(hf, None, p2), at(hf, p1, shift(p2, d)), idx).start()
                to_partner(hf, place(hf, None, p2), 0).start()
                if last:
                    place_out(hf, core, p2, 0).start()
        yield 0.1, 2.8 * part, 2.2, True
        with jax.named_scope(f'gather2_{l}{b}'):
            for hf in range(2):
                p1, p2 = pos(hf)
                src = shift(p2, -sgn)
                line = place(hf, None, src)
                wait_bytes(line, ag_rsem.at[b, hf, 3 + core])
                copy(hf, line, at(hf, p1, shift(p2, sgn)), 5).start()
                to_partner(hf, line, 1).start()
                if last:
                    place_out(hf, core, src, 1).start()
        yield 0.1, 1.4 * part, 0, True
        with jax.named_scope(f'gather3_{l}{b}'):
            for hf in range(2):
                p1, p2 = pos(hf)
                line = place(hf, None, shift(p2, sgn))
                wait_bytes(line, ag_rsem.at[b, hf, 4 - core])
                to_partner(hf, line, 2).start()
                if last:
                    place_out(hf, core, shift(p2, sgn), 2).start()
        yield 0, 0, 2.2, True
        with jax.named_scope(f'gather4_{l}{b}'):
            for hf in range(2):
                p1, p2 = pos(hf)
                line = place(hf, None, shift(p2, 2))
                wait_bytes(line, ag_rsem.at[b, hf, 5])
                to_partner(hf, line, 3).start()
                if last:
                    place_out(hf, core, shift(p2, 2), 3).start()
        yield 0, 0, 1.2, True
        with jax.named_scope(f'gather5_{l}{b}'):
            for hf in range(2):
                p1, p2 = pos(hf)
                for idx, d in enumerate((0, sgn, -sgn, 2)):
                    wait_bytes(place(hf, None, p2), d_rsem.at[b, hf, idx])
                    if last:
                        place_out(hf, other, shift(p2, d), 4 + idx).start()
                for idx in range(3):
                    wait_bytes(place(hf, p1, p2), ag_ssem.at[b, hf, idx])
                for idx in range(3, 6):
                    wait_bytes(place(hf, None, p2), ag_ssem.at[b, hf, idx])
                for idx in range(4):
                    wait_bytes(place(hf, None, p2), d_ssem.at[b, hf, idx])
        if last:
            finals.append(lambda: [place_out(hf, core, shift(pos(hf)[1], 0), idx).wait() for hf in range(2) for idx in range(8)])

    finals = []

    chains = {b: chain(b) for b in range(BLOCKS)}
    ready, light = [0.0] * BLOCKS, [False] * BLOCKS
    now = free = 0.0
    turn = [0, 0]
    while chains:
        if turn:
            b = turn.pop()
        else:
            b = min(chains, key=lambda c: (max(ready[c], now), not light[c], c))
        step = next(chains[b], None)
        if step is None:
            del chains[b]
            continue
        spent, link, delay, light[b] = step
        now = max(now, ready[b]) + spent
        if link:
            free = max(free, now) + link
            ready[b] = free + delay
        else:
            ready[b] = now + delay
    for fin in finals:
        fin()
    for l in range(layers):
        for cp in od_partner(l):
            cp.wait_send()
    for b in range(BLOCKS):
        for i in range(2):
            h_send(b, i).wait_send()
            for k in range(1, side):
                p1_copy(b, i, k).wait_send()
                p2_copy(b, i, k).wait_send()
        if layers > 1:
            st_copy(b).wait_send()


def solution(mesh):
    tp_size = mesh.shape['tp']
    side = math.isqrt(tp_size // 2)
    arg_specs = (P('dp', None), P('dp'), P(), P(None, None, 'tp'), P(None, None, 'tp'), P(None, None, 'tp'), P(None, 'tp', None), P(None, None, 'tp'), P(None, None, 'tp'), P(None, 'tp', None), P(None, 'dp', None, 'tp', None), P(None, 'dp', None, 'tp', None))

    def per_device(x_in, lengths, norm_gain, w_q, w_k, w_v, w_o, w_gate, w_up, w_down, k_cache, v_cache):
        tok_rows, width = x_in.shape
        layers, _, head = w_q.shape
        ff = w_gate.shape[2]
        seq = k_cache.shape[2]
        chips = side * side
        rows = tok_rows // BLOCKS
        toks = rows // chips
        half = width // 2
        ff_tiles = -(-ff // head)
        kdim = head * (1 + ff_tiles)

        inv_freq = (1.0 / (ROPE_BASE ** (np.arange(0, head, 2, dtype=np.float64) / head))).astype(np.float32)
        freq = jnp.asarray(np.concatenate([inv_freq, inv_freq])[None, :])

        any_spec = pl.BlockSpec(memory_space=pl.ANY)
        dma = pltpu.SemaphoreType.DMA
        out = pl.pallas_call(
            functools.partial(layers_kernel, side),
            out_shape=jax.ShapeDtypeStruct((BLOCKS, side, side, toks, width), BF16),
            in_specs=[any_spec] * 13,
            out_specs=any_spec,
            scratch_shapes=[
                pltpu.VMEM((tok_rows // 128, 128), jnp.int32),
                pltpu.VMEM((1, head), F32),
                pltpu.VMEM((layers, width), BF16),
                pltpu.VMEM((BLOCKS, side, side, toks, width), BF16),
                pltpu.VMEM((tok_rows, 1), jnp.int32),
                pltpu.VMEM((tok_rows, head), F32),
                pltpu.VMEM((tok_rows, head), F32),
                pltpu.VMEM((BLOCKS, rows, 16 * seq), F32),
                pltpu.VMEM((BLOCKS, rows, 16 * seq), BF16),
                pltpu.VMEM((BLOCKS, rows, 1), F32),
                pltpu.VMEM((BLOCKS, side, side, toks, width), BF16),
                pltpu.VMEM((layers, width, 3 * head), BF16),
                pltpu.VMEM((layers, ff_tiles * TILE, width), BF16),
                pltpu.VMEM((layers, 2 * kdim, half), BF16),
                pltpu.VMEM((BLOCKS, rows * seq, head), BF16),
                pltpu.VMEM((BLOCKS, rows * seq, head), BF16),
                pltpu.VMEM((BLOCKS, rows, head), BF16),
                pltpu.VMEM((BLOCKS, rows, head), BF16),
                pltpu.VMEM((BLOCKS, rows, 1), F32),
                pltpu.VMEM((BLOCKS, 2, rows, kdim), BF16),
                pltpu.VMEM((BLOCKS, side, side, toks, half), BF16),
                pltpu.VMEM((BLOCKS, 2, side - 1, side, toks, half // 2), BF16),
                pltpu.VMEM((BLOCKS, 2, side, toks, half // 2), F32),
                pltpu.VMEM((BLOCKS, 2, side - 1, toks, half // 2), F32),
                pltpu.VMEM((BLOCKS, toks, half), BF16),
                pltpu.VMEM((BLOCKS, toks, 128), F32),
                pltpu.VMEM((BLOCKS, toks, 128), F32),
                dma((3,)),
                dma((BLOCKS,)),
                dma((layers, 3 + 2 * ff_tiles)),
                dma((layers, 2)),
                dma((layers, 2)),
                dma((layers, 2)),
                dma((BLOCKS, 2)),
                dma((BLOCKS,)),
                dma((BLOCKS, 2)),
                dma((BLOCKS, 2)),
                dma((BLOCKS, 2, side - 1)),
                dma((BLOCKS, 2, side - 1)),
                dma((BLOCKS, 2, side - 1)),
                dma((BLOCKS, 2, side - 1)),
                dma((BLOCKS, 2)),
                dma((BLOCKS, 2, 6)),
                dma((BLOCKS, 2, 6)),
                dma((BLOCKS, 2, 4)),
                dma((BLOCKS, 2, 4)),
                dma((BLOCKS, 2, 8)),
            ],
            compiler_params=pltpu.CompilerParams(collective_id=0, has_side_effects=True, vmem_limit_bytes=67043328),
            name='decoder_layers',
        )(
            x_in.reshape(BLOCKS, side, side, toks, width),
            lengths.reshape(tok_rows // 128, 128),
            freq,
            norm_gain,
            w_q, w_k, w_v, w_o,
            w_gate.swapaxes(1, 2),
            w_up.swapaxes(1, 2),
            w_down,
            k_cache.reshape(layers, tok_rows * seq, head),
            v_cache.reshape(layers, tok_rows * seq, head),
        )
        return out.reshape(tok_rows, width)

    return jax.shard_map(per_device, mesh=mesh, in_specs=arg_specs, out_specs=P('dp', None), check_vma=False)
```

time: 164 us -> 115 us (0.70)
  Pallas kernels: 154 us -> 110 us
  local copies, waits for them, and re-layouts: 7.57 us -> 4.7 us
  other arithmetic: 2.69 us -> 0 us
    pallas_call x1, Pallas kernels: 154 us -> 110 us  [per_device(): pl.pallas_call(functools.partial(layers_kernel, side), out_shape=jax.Shap...]
    reshape x2 -> x0, local copies, waits for them, and re-layouts: 2.87 us -> none  [the longest x1 1.53 us: per_device(): lengths.reshape(tok_rows, 1)]
where the time goes in v1:
time: 115 us
  Pallas kernels  110 us (96%)
  local copies, waits for them, and re-layouts  4.7 us (4%)
    pallas_call x1, Pallas kernels, per_device(): pl.pallas_call(functools.partial(layers_kernel, side), out_shape=jax.Shap...  110 us
    unnamed x1, local copies, waits for them, and re-layouts  4.7 us

profile of v1, /device:TPU:97, one launch (start us, length us, event | category | flops | bytes accessed | tf_op | source)
XLA Modules:
  0.0 114.6 jit_solution(15555744274744515564)
XLA Ops:
  0.0 109.9 %decoder_layers.1 = bf16[2,4,4,16,4096]{4,3,2,1,0:T(8,128)(2,1)} custom-call(bf16[2,4,4,16,4096]{4,3,2,1,0:T(8,128)(2,1)} %bitcast.12, s32[4,128]{1,0:T(4,128)} %bitcast.13, f32[1,128]{1,0:T(1,128)} %constant.2.clone.freq_hbm, bf16[2,4096]{1,0:T(2,128)(2,1)} %gain_hbm.1, bf16[2,4096,128]{2,1,0:T(8,128)(2,1)} %wq.1, bf16[2,4096,128]{2,1,0:T(8,128)(2,1)} %wk.1, ...), custom_call_target="tpu_custom_call" | custom-call | tf_op jit(solution)/shard_map/decoder_layers/pallas_call | solution.py:499
  109.9 4.7 %copy.15 = bf16[512,4096]{1,0:T(8,128)(2,1)} copy(bf16[512,4096]{1,0:T(8,128)(2,1)} %bitcast.7) | data formatting | bytes 8388608

commit v2 on v1

--- a/solution.py
+++ b/solution.py
@@ -15,6 +15,7 @@
 BF16 = jnp.bfloat16
 NT = (((1,), (1,)), ((), ()))
 BLOCKS = 2
+WIRE = 1.0
 TILE = 256
 
 
@@ -22,9 +23,9 @@
     pltpu.make_async_copy(ref, ref, sem).wait()
 
 
-def layers_kernel(side, x_hbm, len_hbm, freq_hbm, gain_hbm, wq, wk, wv, wo, wg, wu, wd, kc, vc, out_hbm,
-                  len_in, freq_ref, gain_ref, out_ref, len_ref, cos_ref, sin_ref, lg_s, pr_s, ow_s, a_buf, wqkv, wgu, wod, kbuf, vbuf, q_s, v_s, self_s, h_buf, send, r1, mid, r2, x_own, st_send, st_recv,
-                  small_sem, x_sem, w_sem, wo_sem, wp_ssem, wp_rsem, c_sem, own_sem, h_ssem, h_rsem, p1_ssem, p1_rsem, p2_ssem, p2_rsem, st_sem, ag_ssem, ag_rsem, d_ssem, d_rsem, out_sem):
+def layers_kernel(side, x_hbm, len_hbm, freq_hbm, gain_hbm, wq, wk, wv, wo, wg, wu, wd, kc, vc, out_ref,
+                  len_in, freq_ref, gain_ref, len_ref, cos_ref, sin_ref, lg_s, pr_s, ow_s, a_buf, wqkv, wgu, wod, kbuf, vbuf, q_s, v_s, self_s, h_buf, send, r1, mid, r2, x_own, st_send, st_recv,
+                  small_sem, x_sem, w_sem, wo_sem, wp_ssem, wp_rsem, c_sem, own_sem, h_ssem, h_rsem, p1_ssem, p1_rsem, p2_ssem, p2_rsem, st_sem, ag_ssem, ag_rsem, d_ssem, d_rsem):
     layers, width = wq.shape[0], wq.shape[1]
     head = wq.shape[2]
     ff = wd.shape[1]
@@ -113,7 +114,7 @@
             inv = lax.rsqrt(jnp.mean(xv * xv, axis=-1, keepdims=True) + NORM_EPS)
             a_buf[b, y, x] = (xv * inv * gain_ref[0:1, :].astype(F32)).astype(BF16)
             return carry
-        lax.fori_loop(0, chips, body, 0, unroll=2)
+        lax.fori_loop(0, chips, body, 0, unroll=4)
 
     tail = ff - (ff_tiles - 1) * head
     with jax.named_scope('zeros'):
@@ -127,11 +128,7 @@
     pl.semaphore_signal(bar, inc=1, device_id=partner)
     for k in range(1, chips):
         pl.semaphore_signal(bar, inc=1, device_id=dev(shift(py, k // side), shift(px, k % side), core))
-    with jax.named_scope('wait_x'):
-        wait(smalls + [x_load(0)])
-    start(gu_loads(0) + cache_loads(0, 0) + od_own(0))
-    with jax.named_scope('norm_00'):
-        norm_rows(0)
+    wait(smalls)
     with jax.named_scope('tables'):
         lane = lax.broadcasted_iota(jnp.int32, (128, head), 1)
         for i in range(len_in.shape[0]):
@@ -141,7 +138,11 @@
             cos_ref[i * 128:(i + 1) * 128, :] = jnp.cos(angle)
             sin = jnp.sin(angle)
             sin_ref[i * 128:(i + 1) * 128, :] = jnp.where(lane < head // 2, -sin, sin)
-
+    with jax.named_scope('wait_x'):
+        wait([x_load(0)])
+    start(gu_loads(0) + cache_loads(0, 0) + od_own(0))
+    with jax.named_scope('norm_00'):
+        norm_rows(0)
     def enter():
         with jax.named_scope('barrier'):
             pl.semaphore_wait(bar, chips)
@@ -169,6 +170,7 @@
             with jax.named_scope(f'norm_{l}{b}'):
                 wait([x_load(b)])
                 norm_rows(b)
+            yield 1.4 * part, 0, 0, False
         r0 = b * rows
         with jax.named_scope(f'qkv_{l}{b}'):
             a = a_buf[b].reshape(rows, width)
@@ -183,7 +185,7 @@
             q_s[b] = qr
             v_s[b] = qkv[:, 2 * head:]
             self_s[b] = jnp.sum(qr.astype(F32) * kr.astype(F32), axis=-1, keepdims=True) * scale
-        yield 1.5 * part + (1.5 * part if l == 0 else 0), 0, 0, False
+        yield 1.5 * part, 0, 0, False
         if l == 0 and b == 0:
             enter()
         with jax.named_scope(f'wait_gu_{l}{b}'):
@@ -205,7 +207,6 @@
             wait(cache_loads(l, b))
         grp = 16
         unroll = 4
-        span = 64
 
         def group(g):
             return pl.ds(pl.multiple_of(g * grp, grp), grp), pl.ds(pl.multiple_of(g * grp * seq, grp * seq), grp * seq)
@@ -216,20 +217,17 @@
                 lg_s[b, sl, :] = lax.dot_general(q_s[b, sl, :], kbuf[b, ks, :], NT, preferred_element_type=F32)
             return carry
 
-        def soften(i, carry):
-            sl = pl.ds(pl.multiple_of(i * span, span), span)
-            lens = len_ref[pl.ds(pl.multiple_of(r0 + i * span, span), span), :]
-            row_id = lax.rem(lax.broadcasted_iota(jnp.int32, (span, grp * seq), 0), grp)
-            dist = lax.broadcasted_iota(jnp.int32, (span, grp * seq), 1) - row_id * seq
-            logits = jnp.where((dist >= 0) & (dist < lens), lg_s[b, sl, :] * scale, -jnp.inf)
-            own = self_s[b, sl, :]
+        def soften():
+            row_id = lax.rem(lax.broadcasted_iota(jnp.int32, (rows, grp * seq), 0), grp)
+            dist = lax.broadcasted_iota(jnp.int32, (rows, grp * seq), 1) - row_id * seq
+            logits = jnp.where((dist >= 0) & (dist < len_ref[r0:r0 + rows, :]), lg_s[b] * scale, -jnp.inf)
+            own = self_s[b]
             peak = jnp.maximum(jnp.max(logits, axis=-1, keepdims=True), own)
             w = jnp.exp(logits - peak)
             own_w = jnp.exp(own - peak)
             inv = 1.0 / (jnp.sum(w, axis=-1, keepdims=True) + own_w)
-            pr_s[b, sl, :] = (w * inv).astype(BF16)
-            ow_s[b, sl, :] = (own_w * inv).astype(BF16).astype(F32)
-            return carry
+            pr_s[b] = (w * inv).astype(BF16)
+            ow_s[b] = (own_w * inv).astype(BF16).astype(F32)
 
         def mix(i, carry):
             for u in range(unroll):
@@ -241,13 +239,13 @@
         with jax.named_scope(f'score_{l}{b}'):
             lax.fori_loop(0, rows // grp // unroll, score, 0)
         with jax.named_scope(f'soften_{l}{b}'):
-            lax.fori_loop(0, rows // span, soften, 0)
+            soften()
         with jax.named_scope(f'mix_{l}{b}'):
             lax.fori_loop(0, rows // grp // unroll, mix, 0)
         h_send(b, 0).start()
         if l + 1 < layers:
             start(cache_loads(l + 1, b))
-        yield 3.4 * part, 0, 1.5, False
+        yield 2.2 * part, 0, 1.5, False
         with jax.named_scope(f'wait_down_{l}{b}'):
             if b == 0:
                 wait(od_own(l))
@@ -368,11 +366,6 @@
         def copy(hf, ref, target, idx):
             return pltpu.make_async_remote_copy(ref, ref, ag_ssem.at[b, hf, idx], ag_rsem.at[b, hf, idx], device_id=target)
 
-        def place_out(hf, c, p2, idx):
-            y, x = (p2, slice(None)) if hf == 0 else (slice(None), p2)
-            cols = part_cols(hf, c)
-            return pltpu.make_async_copy(buf.at[b, y, x, :, cols], out_hbm.at[b, y, x, :, cols], out_sem.at[b, hf, idx])
-
         def to_partner(hf, ref, idx):
             return pltpu.make_async_remote_copy(ref, ref, d_ssem.at[b, hf, idx], d_rsem.at[b, hf, idx], device_id=partner)
 
@@ -389,8 +382,6 @@
                 for idx, d in ((3, 1), (4, -1)):
                     copy(hf, place(hf, None, p2), at(hf, p1, shift(p2, d)), idx).start()
                 to_partner(hf, place(hf, None, p2), 0).start()
-                if last:
-                    place_out(hf, core, p2, 0).start()
         yield 0.1, 2.8 * part, 2.2, True
         with jax.named_scope(f'gather2_{l}{b}'):
             for hf in range(2):
@@ -400,8 +391,6 @@
                 wait_bytes(line, ag_rsem.at[b, hf, 3 + core])
                 copy(hf, line, at(hf, p1, shift(p2, sgn)), 5).start()
                 to_partner(hf, line, 1).start()
-                if last:
-                    place_out(hf, core, src, 1).start()
         yield 0.1, 1.4 * part, 0, True
         with jax.named_scope(f'gather3_{l}{b}'):
             for hf in range(2):
@@ -409,8 +398,6 @@
                 line = place(hf, None, shift(p2, sgn))
                 wait_bytes(line, ag_rsem.at[b, hf, 4 - core])
                 to_partner(hf, line, 2).start()
-                if last:
-                    place_out(hf, core, shift(p2, sgn), 2).start()
         yield 0, 0, 2.2, True
         with jax.named_scope(f'gather4_{l}{b}'):
             for hf in range(2):
@@ -418,27 +405,18 @@
                 line = place(hf, None, shift(p2, 2))
                 wait_bytes(line, ag_rsem.at[b, hf, 5])
                 to_partner(hf, line, 3).start()
-                if last:
-                    place_out(hf, core, shift(p2, 2), 3).start()
         yield 0, 0, 1.2, True
         with jax.named_scope(f'gather5_{l}{b}'):
             for hf in range(2):
                 p1, p2 = pos(hf)
-                for idx, d in enumerate((0, sgn, -sgn, 2)):
+                for idx in range(4):
                     wait_bytes(place(hf, None, p2), d_rsem.at[b, hf, idx])
-                    if last:
-                        place_out(hf, other, shift(p2, d), 4 + idx).start()
                 for idx in range(3):
                     wait_bytes(place(hf, p1, p2), ag_ssem.at[b, hf, idx])
                 for idx in range(3, 6):
                     wait_bytes(place(hf, None, p2), ag_ssem.at[b, hf, idx])
                 for idx in range(4):
                     wait_bytes(place(hf, None, p2), d_ssem.at[b, hf, idx])
-        if last:
-            finals.append(lambda: [place_out(hf, core, shift(pos(hf)[1], 0), idx).wait() for hf in range(2) for idx in range(8)])
-
-    finals = []
-
     chains = {b: chain(b) for b in range(BLOCKS)}
     ready, light = [0.0] * BLOCKS, [False] * BLOCKS
     now = free = 0.0
@@ -455,12 +433,10 @@
         spent, link, delay, light[b] = step
         now = max(now, ready[b]) + spent
         if link:
-            free = max(free, now) + link
+            free = max(free, now) + link * WIRE
             ready[b] = free + delay
         else:
             ready[b] = now + delay
-    for fin in finals:
-        fin()
     for l in range(layers):
         for cp in od_partner(l):
             cp.wait_send()
@@ -498,14 +474,13 @@
         dma = pltpu.SemaphoreType.DMA
         out = pl.pallas_call(
             functools.partial(layers_kernel, side),
-            out_shape=jax.ShapeDtypeStruct((BLOCKS, side, side, toks, width), BF16),
+            out_shape=pltpu.VMEM((BLOCKS, side, side, toks, width), BF16),
             in_specs=[any_spec] * 13,
-            out_specs=any_spec,
+            out_specs=pl.BlockSpec(memory_space=pltpu.VMEM),
             scratch_shapes=[
                 pltpu.VMEM((tok_rows // 128, 128), jnp.int32),
                 pltpu.VMEM((1, head), F32),
                 pltpu.VMEM((layers, width), BF16),
-                pltpu.VMEM((BLOCKS, side, side, toks, width), BF16),
                 pltpu.VMEM((tok_rows, 1), jnp.int32),
                 pltpu.VMEM((tok_rows, head), F32),
                 pltpu.VMEM((tok_rows, head), F32),
@@ -548,9 +523,8 @@
                 dma((BLOCKS, 2, 6)),
                 dma((BLOCKS, 2, 4)),
                 dma((BLOCKS, 2, 4)),
-                dma((BLOCKS, 2, 8)),
             ],
-            compiler_params=pltpu.CompilerParams(collective_id=0, has_side_effects=True, vmem_limit_bytes=67043328),
+            compiler_params=pltpu.CompilerParams(collective_id=0, has_side_effects=True, vmem_limit_bytes=58 * 2**20),
             name='decoder_layers',
         )(
             x_in.reshape(BLOCKS, side, side, toks, width),

time: 115 us -> 105 us (0.913)
  Pallas kernels: 110 us -> 103 us
  local copies, waits for them, and re-layouts: 4.7 us -> 2.02 us
    pallas_call x1, Pallas kernels: 110 us -> 103 us  [per_device(): pl.pallas_call(functools.partial(layers_kernel, side), out_shape=pltpu.VM...]
    unnamed x1, local copies, waits for them, and re-layouts: 4.7 us -> 2.02 us
where the time goes in v2:
time: 105 us
  Pallas kernels  103 us (98%)
  local copies, waits for them, and re-layouts  2.02 us (2%)
    pallas_call x1, Pallas kernels, per_device(): pl.pallas_call(functools.partial(layers_kernel, side), out_shape=pltpu.VM...  103 us

profile of v2, /device:TPU:97, one launch (start us, length us, event | category | flops | bytes accessed | tf_op | source)
XLA Modules:
  0.0 104.8 jit_solution(13671561629728147355)
XLA Ops:
  0.0 102.7 %decoder_layers.1 = bf16[2,4,4,16,4096]{4,3,2,1,0:T(8,128)(2,1)S(1)} custom-call(bf16[2,4,4,16,4096]{4,3,2,1,0:T(8,128)(2,1)} %bitcast.12, s32[4,128]{1,0:T(4,128)} %bitcast.13, f32[1,128]{1,0:T(1,128)} %constant.2.clone.freq_hbm, bf16[2,4096]{1,0:T(2,128)(2,1)} %gain_hbm.1, bf16[2,4096,128]{2,1,0:T(8,128)(2,1)} %wq.1, bf16[2,4096,128]{2,1,0:T(8,128)(2,1)} %wk.1, ...), custom_call_target="tpu_custom_call" | custom-call | tf_op jit(solution)/shard_map/decoder_layers/pallas_call | solution.py:475
  102.7 2.0 %copy.15 = bf16[512,4096]{1,0:T(8,128)(2,1)} copy(bf16[512,4096]{1,0:T(8,128)(2,1)S(1)} %bitcast.7) | data formatting | bytes 8388608

commit v3 on v2

--- a/solution.py
+++ b/solution.py
@@ -15,7 +15,8 @@
 BF16 = jnp.bfloat16
 NT = (((1,), (1,)), ((), ()))
 BLOCKS = 2
-WIRE = 1.0
+SUBS = 2
+WIRE = 1.1
 TILE = 256
 
 
@@ -33,7 +34,7 @@
     quarter = width // 4
     toks = x_hbm.shape[3]
     chips = side * side
-    rows = chips * toks
+    rows = SUBS * chips * toks
     seq = kc.shape[1] // (BLOCKS * rows)
     ff_tiles = wgu.shape[1] // TILE
     kdim = h_buf.shape[3]
@@ -62,8 +63,11 @@
     def k_rows(c, start, n):
         return pl.ds(pl.multiple_of(c * kdim + start, 8), n)
 
+    def subs(b):
+        return pl.ds(b * SUBS, SUBS)
+
     def x_load(b):
-        return pltpu.make_async_copy(x_hbm.at[b], out_ref.at[b], x_sem.at[b])
+        return pltpu.make_async_copy(x_hbm.at[subs(b)], out_ref.at[subs(b)], x_sem.at[b])
 
     def qkv_loads(l):
         return [pltpu.make_async_copy(w.at[l], wqkv.at[l, :, pl.ds(i * head, head)], w_sem.at[l, i]) for i, w in enumerate((wq, wk, wv))]
@@ -109,12 +113,14 @@
 
     def norm_rows(b):
         def body(i, carry):
-            y, x = lax.div(i, side), lax.rem(i, side)
-            xv = out_ref[b, y, x].astype(F32)
+            sb = b * SUBS + lax.div(i, chips // 2)
+            pair = lax.rem(i, chips // 2)
+            y, x = lax.div(pair, side // 2), pl.ds(lax.rem(pair, side // 2) * 2, 2)
+            xv = out_ref[sb, y, x].astype(F32)
             inv = lax.rsqrt(jnp.mean(xv * xv, axis=-1, keepdims=True) + NORM_EPS)
-            a_buf[b, y, x] = (xv * inv * gain_ref[0:1, :].astype(F32)).astype(BF16)
+            a_buf[sb, y, x] = (xv * inv * gain_ref[0:1, :].astype(F32)).astype(BF16)
             return carry
-        lax.fori_loop(0, chips, body, 0, unroll=4)
+        lax.fori_loop(0, SUBS * chips // 2, body, 0, unroll=4)
 
     tail = ff - (ff_tiles - 1) * head
     with jax.named_scope('zeros'):
@@ -152,15 +158,19 @@
 
     for b in range(1, BLOCKS):
         start([x_load(b)] + cache_loads(0, b))
-    for b in range(BLOCKS):
+    for b in range(BLOCKS * SUBS):
         start([pltpu.make_async_copy(x_hbm.at[b, py, px, :, my_cols], x_own.at[b], own_sem.at[b])])
 
     part = rows / 256
-
-    def chain(b):
+    share = part / SUBS
+
+    def compute_chain(b):
         for l in range(layers):
             yield from compute(l, b)
-            yield from finish(l, b)
+
+    def finish_chain(sb):
+        for l in range(layers):
+            yield from finish(l, sb)
 
     def compute(l, b):
         if b == 0:
@@ -173,7 +183,7 @@
             yield 1.4 * part, 0, 0, False
         r0 = b * rows
         with jax.named_scope(f'qkv_{l}{b}'):
-            a = a_buf[b].reshape(rows, width)
+            a = a_buf[subs(b)].reshape(rows, width)
             qkv = jnp.dot(a, wqkv[l], preferred_element_type=F32).astype(BF16)
             cosv, sinv = cos_ref[r0:r0 + rows, :], sin_ref[r0:r0 + rows, :]
 
@@ -196,7 +206,7 @@
                 h_send(b, i).wait_send()
         for j in range(ff_tiles):
             with jax.named_scope(f'gu_{l}{b}'):
-                gu = lax.dot_general(a_buf[b].reshape(rows, width), wgu[l, j * TILE:(j + 1) * TILE, :], NT, preferred_element_type=F32)
+                gu = lax.dot_general(a_buf[subs(b)].reshape(rows, width), wgu[l, j * TILE:(j + 1) * TILE, :], NT, preferred_element_type=F32)
                 gate = gu[:, :head].astype(BF16).astype(F32)
                 up = gu[:, head:].astype(BF16).astype(F32)
                 h_buf[b, core, :, (j + 1) * head:(j + 2) * head] = (gate * jax.nn.sigmoid(gate) * up).astype(BF16)
@@ -255,16 +265,18 @@
                 h_send(b, i).wait_recv()
         for hf in range(2):
             with jax.named_scope(f'down_{l}{b}'):
-                if l > 0:
-                    for k in range(1, side):
-                        p1_copy(b, hf, k).wait_send()
+                if l > 0 and hf == 0:
+                    for sb in range(b * SUBS, (b + 1) * SUBS):
+                        wait_bytes(r1.at[sb], p1_ssem.at[sb])
                 for j in range(hf * quarter // TILE, (hf + 1) * quarter // TILE):
                     cols = slice(j * TILE, (j + 1) * TILE)
                     y = jnp.dot(h_buf[b, 0], wod[l, 0:kdim, cols], preferred_element_type=F32) + jnp.dot(h_buf[b, 1], wod[l, kdim:2 * kdim, cols], preferred_element_type=F32)
-                    send[b, :, :, :, cols] = y.astype(BF16).reshape(side, side, toks, TILE)
-                for k in far_first:
-                    p1_copy(b, hf, k).start()
-        yield 1.8 * part, 5.6 * part, 2.2, True
+                    send[subs(b), :, :, :, cols] = y.astype(BF16).reshape(SUBS, side, side, toks, TILE)
+                for sb in range(b * SUBS, (b + 1) * SUBS):
+                    for k in far_first:
+                        p1_copy(sb, hf, k).start()
+        needs = [('rows', l, sb) for sb in range(b * SUBS, (b + 1) * SUBS)]
+        yield 1.8 * part, 0, 0, False, needs, [(('shares', l, sb), 5.6 * share, 2.2) for sb in range(b * SUBS, (b + 1) * SUBS)]
 
     def h_send(b, i):
         ref = h_buf.at[b, core, :, pl.ds(0, head)] if i == 0 else h_buf.at[b, core, :, pl.ds(head, kdim - head)]
@@ -287,12 +299,12 @@
     def p1_copy(b, hf, k):
         p1, p2 = pos(hf)
         to = shift(p1, k)
-        return pltpu.make_async_remote_copy(line_of(send, b, hf, to, hf_cols(hf)), r1.at[b, hf, k - 1], p1_ssem.at[b, hf, k - 1], p1_rsem.at[b, hf, k - 1], device_id=at(hf, to, p2))
+        return pltpu.make_async_remote_copy(line_of(send, b, hf, to, hf_cols(hf)), r1.at[b, hf, k - 1], p1_ssem.at[b], p1_rsem.at[b, hf], device_id=at(hf, to, p2))
 
     def p2_copy(b, hf, k):
         p1, p2 = pos(hf)
         to = shift(p2, k)
-        return pltpu.make_async_remote_copy(mid.at[b, hf, to], r2.at[b, hf, k - 1], p2_ssem.at[b, hf, k - 1], p2_rsem.at[b, hf, k - 1], device_id=at(hf, p1, to))
+        return pltpu.make_async_remote_copy(mid.at[b, hf, to], r2.at[b, hf, k - 1], p2_ssem.at[b], p2_rsem.at[b, hf], device_id=at(hf, p1, to))
 
     def st_copy(b):
         return pltpu.make_async_remote_copy(st_send.at[b], st_recv.at[b], st_sem.at[b, 0], st_sem.at[b, 1], device_id=partner)
@@ -306,10 +318,9 @@
         for hf in range(2):
             p1, p2 = pos(hf)
             with jax.named_scope(f'wait_p1_{l}{b}'):
-                for k in range(1, side):
-                    p1_copy(b, hf, k).wait_recv()
-                    if l > 0:
-                        p2_copy(b, hf, k).wait_send()
+                wait_bytes(r1.at[b, hf], p1_rsem.at[b, hf])
+                if l > 0 and hf == 0:
+                    wait_bytes(r2.at[b], p2_ssem.at[b])
             with jax.named_scope(f'mid_{l}{b}'):
                 for q in range(side):
                     own = send[b, q, p1, :, hf * quarter:(hf + 1) * quarter] if hf == 0 else send[b, p1, q, :, hf * quarter:(hf + 1) * quarter]
@@ -319,13 +330,12 @@
                     mid[b, hf, q] = acc
                 for k in far_first:
                     p2_copy(b, hf, k).start()
-        yield 0.4 * part, 2.8 * part, 2.2, True
+        yield 0.3 * share, 2.8 * share, 2.2, True
         sq = jnp.zeros((toks, 128), F32)
         for hf in range(2):
             p1, p2 = pos(hf)
             with jax.named_scope(f'wait_p2_{l}{b}'):
-                for k in range(1, side):
-                    p2_copy(b, hf, k).wait_recv()
+                wait_bytes(r2.at[b, hf], p2_rsem.at[b, hf])
             with jax.named_scope(f'reduce_{l}{b}'):
                 for c0 in range(0, quarter, chunk):
                     cols = slice(c0, c0 + chunk)
@@ -347,7 +357,7 @@
                 st_copy(b).wait_send()
             st_send[b] = sq
             st_copy(b).start()
-            yield 0.2 * part, 0, 1.4, True
+            yield 0.2 * share, 0, 1.4, True
             with jax.named_scope(f'wait_st_{l}{b}'):
                 st_copy(b).wait_recv()
             with jax.named_scope(f'scale_{l}{b}'):
@@ -364,90 +374,94 @@
             return buf.at[b, y, x, :, part_cols(hf, core)]
 
         def copy(hf, ref, target, idx):
-            return pltpu.make_async_remote_copy(ref, ref, ag_ssem.at[b, hf, idx], ag_rsem.at[b, hf, idx], device_id=target)
-
-        def to_partner(hf, ref, idx):
-            return pltpu.make_async_remote_copy(ref, ref, d_ssem.at[b, hf, idx], d_rsem.at[b, hf, idx], device_id=partner)
+            return pltpu.make_async_remote_copy(ref, ref, ag_ssem.at[b], ag_rsem.at[b, hf, max(idx - 2, 0)], device_id=target)
+
+        def to_partner(ref):
+            return pltpu.make_async_remote_copy(ref, ref, d_ssem.at[b], d_rsem.at[b], device_id=partner)
 
         for idx, d in ((2, 2), (0, 1), (1, -1)):
             for hf in range(2):
                 p1, p2 = pos(hf)
                 copy(hf, place(hf, p1, p2), at(hf, shift(p1, d), p2), idx).start()
-        yield 0.2, 1.4 * part, 2.6, True
+        yield 0.2, 1.4 * share, 2.6, True
         with jax.named_scope(f'gather1_{l}{b}'):
             for hf in range(2):
                 p1, p2 = pos(hf)
-                for idx, d in ((0, -1), (1, 1), (2, 2)):
-                    wait_bytes(place(hf, shift(p1, d), p2), ag_rsem.at[b, hf, idx])
+                wait_bytes(place(hf, pl.ds(0, side - 1), p2), ag_rsem.at[b, hf, 0])
                 for idx, d in ((3, 1), (4, -1)):
                     copy(hf, place(hf, None, p2), at(hf, p1, shift(p2, d)), idx).start()
-                to_partner(hf, place(hf, None, p2), 0).start()
-        yield 0.1, 2.8 * part, 2.2, True
+                to_partner(place(hf, None, p2)).start()
+        yield 0.1, 2.8 * share, 2.2, True
         with jax.named_scope(f'gather2_{l}{b}'):
             for hf in range(2):
                 p1, p2 = pos(hf)
                 src = shift(p2, -sgn)
                 line = place(hf, None, src)
-                wait_bytes(line, ag_rsem.at[b, hf, 3 + core])
+                wait_bytes(line, ag_rsem.at[b, hf, 1 + core])
                 copy(hf, line, at(hf, p1, shift(p2, sgn)), 5).start()
-                to_partner(hf, line, 1).start()
-        yield 0.1, 1.4 * part, 0, True
+                to_partner(line).start()
+        yield 0.1, 1.4 * share, 0, True
         with jax.named_scope(f'gather3_{l}{b}'):
             for hf in range(2):
                 p1, p2 = pos(hf)
                 line = place(hf, None, shift(p2, sgn))
-                wait_bytes(line, ag_rsem.at[b, hf, 4 - core])
-                to_partner(hf, line, 2).start()
+                wait_bytes(line, ag_rsem.at[b, hf, 2 - core])
+                to_partner(line).start()
         yield 0, 0, 2.2, True
         with jax.named_scope(f'gather4_{l}{b}'):
             for hf in range(2):
                 p1, p2 = pos(hf)
                 line = place(hf, None, shift(p2, 2))
-                wait_bytes(line, ag_rsem.at[b, hf, 5])
-                to_partner(hf, line, 3).start()
+                wait_bytes(line, ag_rsem.at[b, hf, 3])
+                to_partner(line).start()
         yield 0, 0, 1.2, True
         with jax.named_scope(f'gather5_{l}{b}'):
-            for hf in range(2):
-                p1, p2 = pos(hf)
-                for idx in range(4):
-                    wait_bytes(place(hf, None, p2), d_rsem.at[b, hf, idx])
-                for idx in range(3):
-                    wait_bytes(place(hf, p1, p2), ag_ssem.at[b, hf, idx])
-                for idx in range(3, 6):
-                    wait_bytes(place(hf, None, p2), ag_ssem.at[b, hf, idx])
-                for idx in range(4):
-                    wait_bytes(place(hf, None, p2), d_ssem.at[b, hf, idx])
-    chains = {b: chain(b) for b in range(BLOCKS)}
-    ready, light = [0.0] * BLOCKS, [False] * BLOCKS
+            wait_bytes(buf.at[b, :, :, :, my_cols], d_rsem.at[b])
+            wait_bytes(buf.at[b, :, :, :, my_cols], d_ssem.at[b])
+            wait_bytes(buf.at[b, pl.ds(0, side - 1), :, :, my_cols], ag_ssem.at[b])
+            wait_bytes(buf.at[b, 0, pl.ds(0, side - 1), :, my_cols], ag_ssem.at[b])
+        yield 0, 0, 0, True, [('shares', l + 1, b)], [(('rows', l, b), 0, 0)]
+
+    chains = {b: compute_chain(b) for b in range(BLOCKS)}
+    chains.update({BLOCKS + sb: finish_chain(sb) for sb in range(BLOCKS * SUBS)})
+    count = len(chains)
+    ready, light = [0.0] * count, [c >= BLOCKS for c in range(count)]
+    needs = [[] if c < BLOCKS else [('shares', 0, c - BLOCKS)] for c in range(count)]
+    known = {}
     now = free = 0.0
     turn = [0, 0]
     while chains:
-        if turn:
-            b = turn.pop()
-        else:
-            b = min(chains, key=lambda c: (max(ready[c], now), not light[c], c))
-        step = next(chains[b], None)
+        able = [c for c in chains if all(n in known for n in needs[c])]
+        begin = {c: max([ready[c], now] + [known[n] for n in needs[c]]) for c in able}
+        c = turn.pop() if turn else min(able, key=lambda c: (begin[c] - (0.7 if c == 0 else 0), not light[c], c))
+        step = next(chains[c], None)
         if step is None:
-            del chains[b]
+            del chains[c]
             continue
-        spent, link, delay, light[b] = step
-        now = max(now, ready[b]) + spent
-        if link:
-            free = max(free, now) + link * WIRE
-            ready[b] = free + delay
-        else:
-            ready[b] = now + delay
+        spent, link, delay, light[c] = step[:4]
+        needs[c], makes = (step[4], step[5]) if len(step) > 4 else ([], [])
+        now = begin[c] + spent
+        for key, wire, late in [(None, link, delay)] + makes:
+            if wire:
+                free = max(free, now) + wire * WIRE
+            at_time = (free if wire else now) + late
+            if key is None:
+                ready[c] = at_time
+            else:
+                known[key] = at_time
+        if needs[c] and needs[c][0][1] >= layers or (c < BLOCKS and needs[c] and needs[c][0][1] == layers - 1):
+            needs[c] = []
     for l in range(layers):
         for cp in od_partner(l):
             cp.wait_send()
     for b in range(BLOCKS):
         for i in range(2):
             h_send(b, i).wait_send()
-            for k in range(1, side):
-                p1_copy(b, i, k).wait_send()
-                p2_copy(b, i, k).wait_send()
+    for sb in range(BLOCKS * SUBS):
+        wait_bytes(r1.at[sb], p1_ssem.at[sb])
+        wait_bytes(r2.at[sb], p2_ssem.at[sb])
         if layers > 1:
-            st_copy(b).wait_send()
+            st_copy(sb).wait_send()
 
 
 def solution(mesh):
@@ -462,7 +476,8 @@
         seq = k_cache.shape[2]
         chips = side * side
         rows = tok_rows // BLOCKS
-        toks = rows // chips
+        parts = BLOCKS * SUBS
+        toks = tok_rows // parts // chips
         half = width // 2
         ff_tiles = -(-ff // head)
         kdim = head * (1 + ff_tiles)
@@ -474,7 +489,7 @@
         dma = pltpu.SemaphoreType.DMA
         out = pl.pallas_call(
             functools.partial(layers_kernel, side),
-            out_shape=pltpu.VMEM((BLOCKS, side, side, toks, width), BF16),
+            out_shape=pltpu.VMEM((parts, side, side, toks, width), BF16),
             in_specs=[any_spec] * 13,
             out_specs=pl.BlockSpec(memory_space=pltpu.VMEM),
             scratch_shapes=[
@@ -487,7 +502,7 @@
                 pltpu.VMEM((BLOCKS, rows, 16 * seq), F32),
                 pltpu.VMEM((BLOCKS, rows, 16 * seq), BF16),
                 pltpu.VMEM((BLOCKS, rows, 1), F32),
-                pltpu.VMEM((BLOCKS, side, side, toks, width), BF16),
+                pltpu.VMEM((parts, side, side, toks, width), BF16),
                 pltpu.VMEM((layers, width, 3 * head), BF16),
                 pltpu.VMEM((layers, ff_tiles * TILE, width), BF16),
                 pltpu.VMEM((layers, 2 * kdim, half), BF16),
@@ -497,13 +512,13 @@
                 pltpu.VMEM((BLOCKS, rows, head), BF16),
                 pltpu.VMEM((BLOCKS, rows, 1), F32),
                 pltpu.VMEM((BLOCKS, 2, rows, kdim), BF16),
-                pltpu.VMEM((BLOCKS, side, side, toks, half), BF16),
-                pltpu.VMEM((BLOCKS, 2, side - 1, side, toks, half // 2), BF16),
-                pltpu.VMEM((BLOCKS, 2, side, toks, half // 2), F32),
-                pltpu.VMEM((BLOCKS, 2, side - 1, toks, half // 2), F32),
-                pltpu.VMEM((BLOCKS, toks, half), BF16),
-                pltpu.VMEM((BLOCKS, toks, 128), F32),
-                pltpu.VMEM((BLOCKS, toks, 128), F32),
+                pltpu.VMEM((parts, side, side, toks, half), BF16),
+                pltpu.VMEM((parts, 2, side - 1, side, toks, half // 2), BF16),
+                pltpu.VMEM((parts, 2, side, toks, half // 2), F32),
+                pltpu.VMEM((parts, 2, side - 1, toks, half // 2), F32),
+                pltpu.VMEM((parts, toks, half), BF16),
+                pltpu.VMEM((parts, toks, 128), F32),
+                pltpu.VMEM((parts, toks, 128), F32),
                 dma((3,)),
                 dma((BLOCKS,)),
                 dma((layers, 3 + 2 * ff_tiles)),
@@ -511,23 +526,23 @@
                 dma((layers, 2)),
                 dma((layers, 2)),
                 dma((BLOCKS, 2)),
-                dma((BLOCKS,)),
+                dma((parts,)),
                 dma((BLOCKS, 2)),
                 dma((BLOCKS, 2)),
-                dma((BLOCKS, 2, side - 1)),
-                dma((BLOCKS, 2, side - 1)),
-                dma((BLOCKS, 2, side - 1)),
-                dma((BLOCKS, 2, side - 1)),
-                dma((BLOCKS, 2)),
-                dma((BLOCKS, 2, 6)),
-                dma((BLOCKS, 2, 6)),
-                dma((BLOCKS, 2, 4)),
-                dma((BLOCKS, 2, 4)),
+                dma((parts,)),
+                dma((parts, 2)),
+                dma((parts,)),
+                dma((parts, 2)),
+                dma((parts, 2)),
+                dma((parts,)),
+                dma((parts, 2, 4)),
+                dma((parts,)),
+                dma((parts,)),
             ],
             compiler_params=pltpu.CompilerParams(collective_id=0, has_side_effects=True, vmem_limit_bytes=58 * 2**20),
             name='decoder_layers',
         )(
-            x_in.reshape(BLOCKS, side, side, toks, width),
+            x_in.reshape(parts, side, side, toks, width),
             lengths.reshape(tok_rows // 128, 128),
             freq,
             norm_gain,

time: 105 us -> 102 us (0.971)
  Pallas kernels: 103 us -> 99.6 us
    pallas_call x1, Pallas kernels: 103 us -> 99.6 us  [per_device(): pl.pallas_call(functools.partial(layers_kernel, side), out_shape=pltpu.VM...]
where the time goes in v3:
time: 102 us
  Pallas kernels  99.6 us (98%)
  local copies, waits for them, and re-layouts  2.02 us (2%)
    pallas_call x1, Pallas kernels, per_device(): pl.pallas_call(functools.partial(layers_kernel, side), out_shape=pltpu.VM...  99.6 us

profile of v3, /device:TPU:97, one launch (start us, length us, event | category | flops | bytes accessed | tf_op | source)
XLA Modules:
  0.0 101.6 jit_solution(15062374611536820394)
XLA Ops:
  0.0 99.6 %decoder_layers.1 = bf16[4,4,4,8,4096]{4,3,2,1,0:T(8,128)(2,1)S(1)} custom-call(bf16[4,4,4,8,4096]{4,3,2,1,0:T(8,128)(2,1)} %bitcast.12, s32[4,128]{1,0:T(4,128)} %bitcast.13, f32[1,128]{1,0:T(1,128)} %constant.2.clone.freq_hbm, bf16[2,4096]{1,0:T(2,128)(2,1)} %gain_hbm.1, bf16[2,4096,128]{2,1,0:T(8,128)(2,1)} %wq.1, bf16[2,4096,128]{2,1,0:T(8,128)(2,1)} %wk.1, ...), custom_call_target="tpu_custom_call" | custom-call | tf_op jit(solution)/shard_map/decoder_layers/pallas_call | solution.py:490
  99.6 2.0 %copy.15 = bf16[512,4096]{1,0:T(8,128)(2,1)} copy(bf16[512,4096]{1,0:T(8,128)(2,1)S(1)} %bitcast.7) | data formatting | bytes 8388608
